TPU v7x, 32 devices: a whole 2x2x4 slice. The times are simulated.
32 devices in a mesh: lat: 4 (over z), lon: 8 (over y, x, core).
Axes of the slice: x: 2, y: 2, z: 4, core: 2. Of those that a mesh axis runs over, the one named last changes fastest.
Arguments:
- grid_latent: bfloat16 [16384, 512], P(('lat', 'lon')), may hold values from -6 to 6
- mesh_latent: bfloat16 [4096, 512], P(('lat', 'lon')), may hold values from -6 to 6
- block_weights: bfloat16 [4, 3, 512, 512], replicated, may hold values from -0.25 to 0.25
- block_gains: float32 [4, 512], replicated, may hold values from 0.5 to 1.5
- grid_cot: bfloat16 [16384, 512], P(('lat', 'lon')), may hold values from -0.046875 to 0.046875
- encode_rows: int32 [32, 32, 4], P(('lat', 'lon')), may hold values from 0 to 511
- encode_senders: int32 [32, 1536], P(('lat', 'lon')), may hold values from 0 to 127, as said below
- encode_receivers: int32 [32, 1536], P(('lat', 'lon')), may hold values from 0 to 127, as said below
- encode_blocks: int32 [32], P(('lat', 'lon')), may hold values from 4 to 12, as said below
- process_rows: int32 [32, 32, 4], P(('lat', 'lon')), may hold values from 0 to 127
- process_senders: int32 [32, 1536], P(('lat', 'lon')), may hold values from 0 to 127, as said below
- process_receivers: int32 [32, 1536], P(('lat', 'lon')), may hold values from 0 to 127, as said below
- process_blocks: int32 [32], P(('lat', 'lon')), may hold values from 4 to 12, as said below
- decode_rows: int32 [32, 32, 4], P(('lat', 'lon')), may hold values from 0 to 127
- decode_senders: int32 [32, 1536], P(('lat', 'lon')), may hold values from 0 to 127, as said below
- decode_receivers: int32 [32, 1536], P(('lat', 'lon')), may hold values from 0 to 511, as said below
- decode_blocks: int32 [32], P(('lat', 'lon')), may hold values from 4 to 12, as said below
Outputs:
- grid_out: bfloat16 [16384, 512], P(('lat', 'lon'))
- weight_grad: bfloat16 [4, 3, 512, 512], replicated
- gain_grad: float32 [4, 512], replicated
Inputs may be any that keep to these rules, and one draw needn't show every extreme that they name: `encode_senders`: on every device each of the 128 received slots is named by some edge of the first 4 blocks. `encode_receivers`: on every device each of its 128 mesh rows is named by some edge of the first 4 blocks. `encode_blocks`: some device has 12 live blocks. `process_senders`: on every device each of the 128 received slots is named by some edge of the first 4 blocks. `process_receivers`: on every device each of its 128 mesh rows is named by some edge of the first 4 blocks. `process_blocks`: some device has 12 live blocks. `decode_senders`: on every device each of the 128 received slots is named by some edge of the first 4 blocks. `decode_receivers`: on every device each of its 512 grid rows is named by some edge of the first 4 blocks. `decode_blocks`: some device has 12 live blocks.
All inputs are finite; a program needn't handle non-finite values.
Results may differ from a plain program's by a relative error of at most 0.017.
Values may be sent and summed in bfloat16 or wider, within the bound.
No kernel may reach another device: no remote copies, remote signals or barrier semaphores. Data moves between devices by JAX's collectives and lax.ppermute only.
A program may use at most 128 MiB of HBM per device.

v0:
```python
import jax
import jax.numpy as jnp
from jax import lax
from jax.sharding import PartitionSpec as P

LAYERS = 2
EDGE_BLOCK = 128
EPSILON = 1e-05


def silu_slope(values):
    sigma = jax.nn.sigmoid(values)
    return sigma * (1.0 + values * (1.0 - sigma))


def transposed_product(left, right):
    return lax.dot_general(
        left, right, (((0,), (0,)), ((), ())), preferred_element_type=jnp.float32
    )


def back_product(grad, weight):
    return lax.dot_general(
        grad, weight, (((1,), (1,)), ((), ())), preferred_element_type=jnp.float32
    )


def projected(latent, weight):
    return jnp.dot(latent, weight, preferred_element_type=jnp.float32).astype(jnp.bfloat16)


def edge_forward(
    slot_vals, proj_recv, latent_recv, senders, receivers, live_mask, weight_out, block_gain
):
    preact = slot_vals[senders].astype(jnp.float32) + proj_recv[receivers].astype(jnp.float32)
    hidden = jax.nn.silu(preact) * live_mask[:, None]
    summed = jax.ops.segment_sum(hidden, receivers, num_segments=proj_recv.shape[0]).astype(
        jnp.bfloat16
    )
    mixed = jnp.dot(summed, weight_out, preferred_element_type=jnp.float32)
    centred = mixed - jnp.mean(mixed, axis=-1, keepdims=True)
    inv_scale = lax.rsqrt(jnp.mean(centred * centred, axis=-1, keepdims=True) + EPSILON)
    normed = centred * inv_scale
    output = (latent_recv.astype(jnp.float32) + normed * block_gain).astype(jnp.bfloat16)
    return (output, preact, summed, normed, inv_scale)


def edge_backward(
    grad_out,
    preact,
    summed,
    normed,
    inv_scale,
    senders,
    receivers,
    live_mask,
    weight_out,
    block_gain,
    recv_count,
    slot_count,
):
    gain_part = jnp.sum(grad_out * normed, axis=0)
    grad_normed = grad_out * block_gain
    grad_mixed = inv_scale * (
        grad_normed
        - jnp.mean(grad_normed, axis=-1, keepdims=True)
        - normed * jnp.mean(grad_normed * normed, axis=-1, keepdims=True)
    )
    grad_mixed = grad_mixed.astype(jnp.bfloat16)
    out_part = transposed_product(summed, grad_mixed)
    grad_summed = back_product(grad_mixed, weight_out)
    grad_pre = grad_summed[receivers] * live_mask[:, None] * silu_slope(preact)
    grad_recv = jax.ops.segment_sum(grad_pre, receivers, num_segments=recv_count).astype(
        jnp.bfloat16
    )
    grad_slots = jax.ops.segment_sum(grad_pre, senders, num_segments=slot_count).astype(
        jnp.bfloat16
    )
    return (grad_recv, grad_slots, out_part, gain_part)


def trade(buffer):
    return lax.all_to_all(buffer, ("lat", "lon"), split_axis=0, concat_axis=0, tiled=True)


def graph_parts(send_rows, senders, receivers, block_count):
    positions = jnp.arange(senders.shape[1], dtype=jnp.int32) // EDGE_BLOCK
    live_mask = (positions < block_count[0]).astype(jnp.float32)
    return (send_rows[0], senders[0], receivers[0], live_mask)


def run_forward(latent_send, latent_recv, weights, block_gain, graph):
    send_rows, senders, receivers, live_mask = graph
    proj_send = projected(latent_send, weights[0])
    outgoing = proj_send[send_rows]
    proj_recv = projected(latent_recv, weights[1])
    slot_vals = trade(outgoing).reshape(-1, proj_send.shape[1])
    output, preact, summed, normed, inv_scale = edge_forward(
        slot_vals, proj_recv, latent_recv, senders, receivers, live_mask, weights[2], block_gain
    )
    return (output, (preact, summed, normed, inv_scale, slot_vals.shape[0]))


def run_backward(grad_out, latent_send, latent_recv, weights, block_gain, graph, saved):
    send_rows, senders, receivers, live_mask = graph
    preact, summed, normed, inv_scale, slot_count = saved
    grad_recv, grad_slots, out_part, gain_part = edge_backward(
        grad_out,
        preact,
        summed,
        normed,
        inv_scale,
        senders,
        receivers,
        live_mask,
        weights[2],
        block_gain,
        latent_recv.shape[0],
        slot_count,
    )
    width = grad_slots.shape[1]
    returned = trade(grad_slots.reshape(send_rows.shape + (width,)))
    grad_send = (
        jnp.zeros((latent_send.shape[0], width), jnp.float32)
        .at[send_rows.reshape(-1)]
        .add(returned.reshape(-1, width).astype(jnp.float32))
        .astype(jnp.bfloat16)
    )
    grad_weights = jnp.stack(
        [
            transposed_product(latent_send, grad_send),
            transposed_product(latent_recv, grad_recv),
            out_part,
        ]
    )
    return (grad_weights, gain_part, grad_send, grad_recv)


def settle(grad_weights, gain_part):
    return (grad_weights, gain_part)


def shards(
    grid_latent,
    mesh_latent,
    block_weights,
    block_gains,
    grid_cot,
    encode_rows,
    encode_senders,
    encode_receivers,
    encode_blocks,
    process_rows,
    process_senders,
    process_receivers,
    process_blocks,
    decode_rows,
    decode_senders,
    decode_receivers,
    decode_blocks,
):
    encode = graph_parts(encode_rows, encode_senders, encode_receivers, encode_blocks)
    process = graph_parts(process_rows, process_senders, process_receivers, process_blocks)
    decode = graph_parts(decode_rows, decode_senders, decode_receivers, decode_blocks)
    latents = [mesh_latent]
    saves = []
    output, saved = run_forward(grid_latent, mesh_latent, block_weights[0], block_gains[0], encode)
    latents.append(output)
    saves.append(saved)
    for layer_id in range(LAYERS):
        current = latents[-1]
        output, saved = run_forward(
            current, current, block_weights[layer_id + 1], block_gains[layer_id + 1], process
        )
        latents.append(output)
        saves.append(saved)
    last_id = LAYERS + 1
    grid_out, decode_saved = run_forward(
        latents[-1], grid_latent, block_weights[last_id], block_gains[last_id], decode
    )
    weight_parts = [None] * (LAYERS + 2)
    gain_parts = [None] * (LAYERS + 2)
    grad_weights, gain_part, grad_send, grad_recv = run_backward(
        grid_cot.astype(jnp.float32),
        latents[-1],
        grid_latent,
        block_weights[last_id],
        block_gains[last_id],
        decode,
        decode_saved,
    )
    weight_parts[last_id], gain_parts[last_id] = settle(grad_weights, gain_part)
    grad_mesh = back_product(grad_send, block_weights[last_id][0])
    for layer_id in reversed(range(LAYERS)):
        block_id = layer_id + 1
        current = latents[block_id]
        grad_weights, gain_part, grad_send, grad_recv = run_backward(
            grad_mesh,
            current,
            current,
            block_weights[block_id],
            block_gains[block_id],
            process,
            saves[block_id],
        )
        weight_parts[block_id], gain_parts[block_id] = settle(grad_weights, gain_part)
        grad_mesh = (
            grad_mesh
            + back_product(grad_recv, block_weights[block_id][1])
            + back_product(grad_send, block_weights[block_id][0])
        )
    grad_weights, gain_part, grad_send, grad_recv = run_backward(
        grad_mesh, grid_latent, mesh_latent, block_weights[0], block_gains[0], encode, saves[0]
    )
    weight_parts[0], gain_parts[0] = settle(grad_weights, gain_part)
    weight_stack = jnp.stack(weight_parts)
    gain_stack = jnp.stack(gain_parts)
    weight_stack, gain_stack = lax.psum((weight_stack, gain_stack), ("lat", "lon"))
    return (grid_out, weight_stack.astype(jnp.bfloat16), gain_stack)


def solution(mesh):
    return jax.shard_map(
        shards,
        mesh=mesh,
        in_specs=(
            P(("lat", "lon"), None),
            P(("lat", "lon"), None),
            P(),
            P(),
            P(("lat", "lon"), None),
            P(("lat", "lon"), None, None),
            P(("lat", "lon"), None),
            P(("lat", "lon"), None),
            P(("lat", "lon")),
            P(("lat", "lon"), None, None),
            P(("lat", "lon"), None),
            P(("lat", "lon"), None),
            P(("lat", "lon")),
            P(("lat", "lon"), None, None),
            P(("lat", "lon"), None),
            P(("lat", "lon"), None),
            P(("lat", "lon")),
        ),
        out_specs=(P(("lat", "lon"), None), P(), P()),
        check_vma=False,
    )
```

profile of v0, /device:TPU:0, one launch (start us, length us, event | category | flops | bytes accessed | tf_op | source)
XLA Modules:
  0.0 602.4 jit_solution(12311952505016923633)
XLA Ops:
  4.9 7.3 %all-to-all-start = ((bf16[32,4,512]{2,1,0:T(4,128)(2,1)}), bf16[32,4,512]{2,1,0:T(4,128)(2,1)S(1)}, u32[]{:S(2)}, u32[]{:S(2)}) async-start(bf16[32,4,512]{2,1,0:T(4,128)(2,1)} %reshape.518), calls=%async_computation | async-start | bytes 262144 | tf_op jit(solution)/shard_map/all_to_all | solution.py:83
  19.4 4.8 gather_fusion.2
  25.8 5.4 gather_fusion.1
  31.2 11.8 %scatter_custom_fusion = f32[128,512]{1,0:T(8,128)S(1)} fusion(s32[1536]{0:T(1024)S(1)} %reduce.1, bf16[1536,512]{1,0:T(8,128)(2,1)S(1)} %gather_fusion.2, bf16[1536,512]{1,0:T(8,128)(2,1)} %gather_fusion.1, f32[1536]{0:T(1024)S(1)} %fusion.133, f32[]{:T(128)} %constant.63.clone.1, f32[]{:T(128)} %constant.59.clone.1), kind=kCustom, calls=%fused_computation.56 | custom fusion | flops 7077888 | bytes 3416072 | tf_op jit(solution)/shard_map/scatter-add | solution.py:37
  48.3 5.8 all-to-all-start.1
  56.2 5.4 gather_fusion.5
  62.3 5.4 gather_fusion.4
  67.8 11.9 %scatter_custom_fusion.1 = f32[128,512]{1,0:T(8,128)S(1)} fusion(s32[1536]{0:T(1024)S(1)} %reduce.4, bf16[1536,512]{1,0:T(8,128)(2,1)} %gather_fusion.5, bf16[1536,512]{1,0:T(8,128)(2,1)} %gather_fusion.4, f32[1536]{0:T(1024)S(1)} %fusion.134, f32[]{:T(128)} %constant.63.clone.1, f32[]{:T(128)} %constant.59.clone.1), kind=kCustom, calls=%fused_computation.51 | custom fusion | flops 7077888 | bytes 3416072 | tf_op jit(solution)/shard_map/scatter-add | solution.py:37
  85.0 5.2 all-to-all-start.2
  92.0 5.4 gather_fusion.8
  98.4 5.4 gather_fusion.7
  103.8 11.7 %scatter_custom_fusion.2 = f32[128,512]{1,0:T(8,128)S(1)} fusion(s32[1536]{0:T(1024)S(1)} %reduce.4, bf16[1536,512]{1,0:T(8,128)(2,1)} %gather_fusion.8, bf16[1536,512]{1,0:T(8,128)(2,1)} %gather_fusion.7, f32[1536]{0:T(1024)S(1)} %fusion.134, f32[]{:T(128)} %constant.63.clone.1, f32[]{:T(128)} %constant.59.clone.1), kind=kCustom, calls=%fused_computation.46 | custom fusion | flops 7077888 | bytes 3416072 | tf_op jit(solution)/shard_map/scatter-add | solution.py:37
  121.4 4.9 all-to-all-start.3
  134.2 2.1 copy.45
  136.2 5.4 gather_fusion.11
  142.3 5.7 gather_fusion.10
  148.0 13.0 %scatter_custom_fusion.3 = f32[512,512]{1,0:T(8,128)} fusion(s32[1536]{0:T(1024)} %reduce, bf16[1536,512]{1,0:T(8,128)(2,1)S(1)} %copy-done.3, bf16[1536,512]{1,0:T(8,128)(2,1)} %gather_fusion.10, f32[1536]{0:T(1024)} %fusion.135, f32[]{:T(128)} %constant.63.clone.1, f32[]{:T(128)} %constant.59.clone.1), kind=kCustom, calls=%fused_computation.41 | custom fusion | flops 7077888 | bytes 4203520 | tf_op jit(solution)/shard_map/scatter-add | solution.py:37
  167.2 4.9 gather_fusion.12
  172.2 4.9 multiply_multiply_fusion.3
  177.0 11.0 %scatter_custom_fusion.4 = f32[128,512]{1,0:T(8,128)} fusion(s32[1536]{0:T(1024)} %reduce.10, f32[1536,512]{1,0:T(8,128)} %multiply_multiply_fusion.3, f32[]{:T(128)} %constant.59.clone.1), kind=kCustom, calls=%fused_computation.206 | custom fusion | flops 786432 | bytes 262656 | tf_op jit(solution)/shard_map/scatter-add | solution.py:76
  189.7 5.8 all-to-all-start.4
  195.5 2.6 convolution_bitcast_fusion
  198.1 10.5 %scatter_custom_fusion.15 = f32[512,512]{1,0:T(8,128)S(1)} fusion(s32[1536]{0:T(1024)} %reduce, f32[1536,512]{1,0:T(8,128)} %multiply_multiply_fusion.3, f32[]{:T(128)} %constant.59.clone.1), kind=kCustom, calls=%fused_computation.141 | custom fusion | flops 786432 | bytes 1049088 | tf_op jit(solution)/shard_map/scatter-add | solution.py:73
  208.6 2.0 copy.56
  220.9 4.9 gather_fusion.13
  225.8 4.5 multiply_multiply_fusion.2
  230.3 10.4 %scatter_custom_fusion.6 = f32[128,512]{1,0:T(8,128)S(1)} fusion(s32[1536]{0:T(1024)} %copy-done.68, f32[1536,512]{1,0:T(8,128)} %multiply_multiply_fusion.2, f32[]{:T(128)} %constant.59.clone.1), kind=kCustom, calls=%fused_computation.202 | custom fusion | flops 786432 | bytes 262656 | tf_op jit(solution)/shard_map/scatter-add | solution.py:73
  240.7 10.3 %scatter_custom_fusion.7 = f32[128,512]{1,0:T(8,128)S(1)} fusion(s32[1536]{0:T(1024)} %reduce.11, f32[1536,512]{1,0:T(8,128)} %multiply_multiply_fusion.2, f32[]{:T(128)} %constant.59.clone.1), kind=kCustom, calls=%fused_computation.200 | custom fusion | flops 786432 | bytes 262656 | tf_op jit(solution)/shard_map/scatter-add | solution.py:76
  251.7 6.0 all-to-all-start.5
  259.0 3.6 maximum_bitcast_fusion.3
  268.6 2.1 multiply_reduce_fusion.2
  274.9 4.9 gather_fusion.14
  279.9 4.5 multiply_multiply_fusion.1
  284.4 10.4 %scatter_custom_fusion.9 = f32[128,512]{1,0:T(8,128)S(1)} fusion(s32[1536]{0:T(1024)} %copy-done.68, f32[1536,512]{1,0:T(8,128)} %multiply_multiply_fusion.1, f32[]{:T(128)} %constant.59.clone.1), kind=kCustom, calls=%fused_computation.196 | custom fusion | flops 786432 | bytes 262656 | tf_op jit(solution)/shard_map/scatter-add | solution.py:73
  294.8 10.3 %scatter_custom_fusion.10 = f32[128,512]{1,0:T(8,128)S(1)} fusion(s32[1536]{0:T(1024)} %reduce.11, f32[1536,512]{1,0:T(8,128)} %multiply_multiply_fusion.1, f32[]{:T(128)} %constant.59.clone.1), kind=kCustom, calls=%fused_computation.194 | custom fusion | flops 786432 | bytes 262656 | tf_op jit(solution)/shard_map/scatter-add | solution.py:76
  305.9 4.0 all-to-all-start.6
  311.3 3.6 maximum_bitcast_fusion.2
  320.8 2.0 multiply_reduce_fusion.3
  327.1 4.9 gather_fusion.15
  332.1 4.4 multiply_multiply_fusion
  336.4 10.5 %scatter_custom_fusion.14 = f32[128,512]{1,0:T(8,128)S(1)} fusion(s32[1536]{0:T(1024)} %copy-done.67, f32[1536,512]{1,0:T(8,128)} %multiply_multiply_fusion, f32[]{:T(128)} %constant.59.clone.1), kind=kCustom, calls=%fused_computation.188 | custom fusion | flops 786432 | bytes 262656 | tf_op jit(solution)/shard_map/scatter-add | solution.py:73
  346.9 10.3 %scatter_custom_fusion.12 = f32[128,512]{1,0:T(8,128)S(1)} fusion(s32[1536]{0:T(1024)} %reduce.9, f32[1536,512]{1,0:T(8,128)} %multiply_multiply_fusion, f32[]{:T(128)} %constant.59.clone.1), kind=kCustom, calls=%fused_computation.190 | custom fusion | flops 786432 | bytes 262656 | tf_op jit(solution)/shard_map/scatter-add | solution.py:76
  357.9 3.9 all-to-all-start.7
  363.9 3.3 maximum_bitcast_fusion.1
  367.3 2.8 all-to-all-done.7
  375.9 6.6 %pad_maximum_fusion = f32[4,3,512,512]{2,3,1,0:T(8,128)} fusion(f32[1,3,512,512]{2,3,1,0:T(8,128)S(1)} %copy-done.4, f32[1,3,512,512]{2,3,1,0:T(8,128)S(1)} %copy-done.5, f32[1,3,512,512]{2,3,1,0:T(8,128)} %maximum_bitcast_fusion.1, f32[1,3,512,512]{2,3,1,0:T(8,128)S(1)} %maximum_bitcast_fusion), kind=kLoop, calls=%fused_computation.32 | loop fusion | flops 9437184 | bytes 25165824 | tf_op jit(solution)/shard_map/stack | solution.py:216
  382.5 210.8 %all-reduce.2 = (bf16[4,3,512,512]{2,3,1,0:T(8,128)(2,1)}, f32[4,512]{1,0:T(4,128)}) all-reduce(f32[4,3,512,512]{2,3,1,0:T(8,128)} %pad_maximum_fusion, f32[4,512]{1,0:T(4,128)S(1)} %pad_maximum_fusion.1), channel_id=1, replica_groups=mesh['lat'=4,'lon'=8] {'lat','lon'}, use_global_device_ids=true, to_apply=%region_32.33 | all-reduce | flops 3147776 | bytes 18890752 | tf_op jit(solution)/shard_map/psum | solution.py:218
  593.3 8.6 %copy.57 = bf16[4,3,512,512]{3,2,1,0:T(8,128)(2,1)} copy(bf16[4,3,512,512]{2,3,1,0:T(8,128)(2,1)} %get-tuple-element.21) | data formatting | bytes 12582912
  (294 shorter events, 91.8 us)
Async XLA Ops:
  0.6 11.6 %copy-start.63 = (s32[1,32,4]{1,2,0:T(4,128)S(1)}, s32[1,32,4]{1,2,0:T(4,128)}, u32[]{:S(2)}) copy-start(s32[1,32,4]{1,2,0:T(4,128)} %param.22) | copy-start | bytes 1540
  0.6 11.7 %copy-start.64 = (s32[1,32,4]{1,2,0:T(4,128)S(1)}, s32[1,32,4]{1,2,0:T(4,128)}, u32[]{:S(2)}) copy-start(s32[1,32,4]{1,2,0:T(4,128)} %param.26) | copy-start | bytes 1540
  0.7 13.7 %copy-start.65 = (s32[1,32,4]{1,2,0:T(4,128)S(1)}, s32[1,32,4]{1,2,0:T(4,128)}, u32[]{:S(2)}) copy-start(s32[1,32,4]{1,2,0:T(4,128)} %param.30) | copy-start | bytes 1540
  0.7 14.4 %copy-start.53 = (s32[1,1536]{1,0:T(1,128)S(1)}, s32[1,1536]{1,0:T(1,128)}, u32[]{:S(2)}) copy-start(s32[1,1536]{1,0:T(1,128)} %param.24) | copy-start | bytes 18436
  0.7 14.4 %copy-start.57 = (s32[1,1536]{1,0:T(1,128)S(1)}, s32[1,1536]{1,0:T(1,128)}, u32[]{:S(2)}) copy-start(s32[1,1536]{1,0:T(1,128)} %param.23) | copy-start | bytes 18436
  0.7 14.5 %copy-start.55 = (s32[1,1536]{1,0:T(1,128)S(1)}, s32[1,1536]{1,0:T(1,128)}, u32[]{:S(2)}) copy-start(s32[1,1536]{1,0:T(1,128)} %param.27) | copy-start | bytes 18436
  0.7 14.5 %copy-start.54 = (s32[1,1536]{1,0:T(1,128)S(1)}, s32[1,1536]{1,0:T(1,128)}, u32[]{:S(2)}) copy-start(s32[1,1536]{1,0:T(1,128)} %param.28) | copy-start | bytes 18436
  0.7 14.6 %copy-start.58 = (s32[1,1536]{1,0:T(1,128)S(1)}, s32[1,1536]{1,0:T(1,128)}, u32[]{:S(2)}) copy-start(s32[1,1536]{1,0:T(1,128)} %param.31) | copy-start | bytes 18436
  0.7 14.6 %copy-start.56 = (s32[1,1536]{1,0:T(1,128)S(1)}, s32[1,1536]{1,0:T(1,128)}, u32[]{:S(2)}) copy-start(s32[1,1536]{1,0:T(1,128)} %param.32) | copy-start | bytes 18436
  0.7 15.2 %copy-start.66 = (f32[4,512]{1,0:T(4,128)S(1)}, f32[4,512]{1,0:T(4,128)}, u32[]{:S(2)}) copy-start(f32[4,512]{1,0:T(4,128)} %param.20) | copy-start | bytes 24580
  0.7 17.4 %copy-start.37 = (bf16[128,512]{1,0:T(8,128)(2,1)S(1)}, bf16[128,512]{1,0:T(8,128)(2,1)}, u32[]{:S(2)}) copy-start(bf16[128,512]{1,0:T(8,128)(2,1)} %param.18) | copy-start | bytes 393220
  4.9 20.8 %all-to-all-start = ((bf16[32,4,512]{2,1,0:T(4,128)(2,1)}), bf16[32,4,512]{2,1,0:T(4,128)(2,1)S(1)}, u32[]{:S(2)}, u32[]{:S(2)}) async-start(bf16[32,4,512]{2,1,0:T(4,128)(2,1)} %reshape.518), calls=%async_computation | async-start | bytes 262144 | tf_op jit(solution)/shard_map/all_to_all | solution.py:83
  14.4 16.8 %copy-start.41 = (f32[1536]{0:T(1024)}, f32[1536]{0:T(1024)S(1)}, u32[]{:S(2)}) copy-start(f32[1536]{0:T(1024)S(1)} %fusion.133) | copy-start | bytes 18436
  15.1 16.1 %copy-start.67 = (s32[1536]{0:T(1024)}, s32[1536]{0:T(1024)S(1)}, u32[]{:S(2)}) copy-start(s32[1536]{0:T(1024)S(1)} %reduce.1) | copy-start | bytes 18436
  16.6 28.1 %copy-start.48 = (f32[1,512]{1,0:T(1,128)}, f32[1,512]{1,0:T(1,128)S(1)}, u32[]{:S(2)}) copy-start(f32[1,512]{1,0:T(1,128)S(1)} %get-tuple-element.27) | copy-start | bytes 6148
  16.6 64.8 %copy-start.50 = (f32[1,512]{1,0:T(1,128)}, f32[1,512]{1,0:T(1,128)S(1)}, u32[]{:S(2)}) copy-start(f32[1,512]{1,0:T(1,128)S(1)} %get-tuple-element.26) | copy-start | bytes 6148
  43.0 18.7 %copy-start.26 = (f32[128,512]{1,0:T(8,128)}, f32[128,512]{1,0:T(8,128)S(1)}, u32[]{:S(2)}) copy-start(f32[128,512]{1,0:T(8,128)S(1)} %scatter_custom_fusion) | copy-start | bytes 786436
  45.4 36.0 %copy-start.33 = (bf16[128,512]{1,0:T(8,128)(2,1)}, bf16[128,512]{1,0:T(8,128)(2,1)S(1)}, u32[]{:S(2)}) copy-start(bf16[128,512]{1,0:T(8,128)(2,1)S(1)} %add_convert_fusion.3) | copy-start | bytes 393220
  48.3 14.0 %all-to-all-start.1 = ((bf16[32,4,512]{2,1,0:T(4,128)(2,1)}), bf16[32,4,512]{2,1,0:T(4,128)(2,1)S(1)}, u32[]{:S(2)}, u32[]{:S(2)}) async-start(bf16[32,4,512]{2,1,0:T(4,128)(2,1)} %reshape.542), calls=%async_computation.1 | async-start | bytes 262144 | tf_op jit(solution)/shard_map/all_to_all | solution.py:83
  54.7 49.1 %copy-start.68 = (s32[1536]{0:T(1024)}, s32[1536]{0:T(1024)S(1)}, u32[]{:S(2)}) copy-start(s32[1536]{0:T(1024)S(1)} %reduce.4) | copy-start | bytes 18436
  79.7 17.8 %copy-start.28 = (f32[128,512]{1,0:T(8,128)}, f32[128,512]{1,0:T(8,128)S(1)}, u32[]{:S(2)}) copy-start(f32[128,512]{1,0:T(8,128)S(1)} %scatter_custom_fusion.1) | copy-start | bytes 786436
  81.1 16.3 %copy-start.71 = (f32[128]{0:T(128)}, f32[128]{0:T(128)S(1)}, u32[]{:S(2)}) copy-start(f32[128]{0:T(128)S(1)} %broadcast_multiply_fusion.10) | copy-start | bytes 1540
  82.1 35.1 %copy-start.35 = (bf16[128,512]{1,0:T(8,128)(2,1)}, bf16[128,512]{1,0:T(8,128)(2,1)S(1)}, u32[]{:S(2)}) copy-start(bf16[128,512]{1,0:T(8,128)(2,1)S(1)} %add_convert_fusion.2) | copy-start | bytes 393220
  85.0 13.4 %all-to-all-start.2 = ((bf16[32,4,512]{2,1,0:T(4,128)(2,1)}), bf16[32,4,512]{2,1,0:T(4,128)(2,1)S(1)}, u32[]{:S(2)}, u32[]{:S(2)}) async-start(bf16[32,4,512]{2,1,0:T(4,128)(2,1)} %reshape.566), calls=%async_computation.2 | async-start | bytes 262144 | tf_op jit(solution)/shard_map/all_to_all | solution.py:83
  103.8 13.9 %copy-start.52 = (f32[1,512]{1,0:T(1,128)S(1)}, f32[1,512]{1,0:T(1,128)}, u32[]{:S(2)}) copy-start(f32[1,512]{1,0:T(1,128)} %get-tuple-element.28) | copy-start | bytes 6148
  115.5 20.7 %copy-start.30 = (f32[128,512]{1,0:T(8,128)}, f32[128,512]{1,0:T(8,128)S(1)}, u32[]{:S(2)}) copy-start(f32[128,512]{1,0:T(8,128)S(1)} %scatter_custom_fusion.2) | copy-start | bytes 786436
  121.4 20.8 %all-to-all-start.3 = ((bf16[32,4,512]{2,1,0:T(4,128)(2,1)}), bf16[32,4,512]{2,1,0:T(4,128)(2,1)S(1)}, u32[]{:S(2)}, u32[]{:S(2)}) async-start(bf16[32,4,512]{2,1,0:T(4,128)(2,1)} %reshape.590), calls=%async_computation.3 | async-start | bytes 262144 | tf_op jit(solution)/shard_map/all_to_all | solution.py:83
  127.1 14.6 %copy-start.46 = (s32[2048]{0:T(1024)}, s32[2048]{0:T(1024)S(1)}, u32[]{:S(2)}) copy-start(s32[2048]{0:T(1024)S(1)} %pad_clamp_fusion) | copy-start | bytes 24580
  148.0 15.2 %copy-start.59 = (f32[1,512]{1,0:T(1,128)S(1)}, f32[1,512]{1,0:T(1,128)}, u32[]{:S(2)}) copy-start(f32[1,512]{1,0:T(1,128)} %get-tuple-element.25) | copy-start | bytes 6148
  172.2 23.3 %copy-start.6 = (f32[512,512]{1,0:T(8,128)S(1)}, f32[512,512]{1,0:T(8,128)}, u32[]{:S(2)}) copy-start(f32[512,512]{1,0:T(8,128)} %scatter_custom_fusion.3) | copy-start | bytes 3145732
  177.0 33.6 %copy-start.12 = (bf16[512,512]{1,0:T(8,128)(2,1)S(1)}, bf16[512,512]{1,0:T(8,128)(2,1)}, u32[]{:S(2)}) copy-start(bf16[512,512]{1,0:T(8,128)(2,1)} %param.17) | copy-start | bytes 1572868
  189.7 22.5 %all-to-all-start.4 = ((bf16[32,4,512]{2,1,0:T(4,128)(2,1)}), bf16[32,4,512]{2,1,0:T(4,128)(2,1)S(1)}, u32[]{:S(2)}, u32[]{:S(2)}) async-start(bf16[32,4,512]{2,1,0:T(4,128)(2,1)} %reshape.509), calls=%async_computation.4 | async-start | bytes 262144 | tf_op jit(solution)/shard_map/all_to_all | solution.py:83
  225.8 31.9 %copy-start.36 = (bf16[128,512]{1,0:T(8,128)(2,1)S(1)}, bf16[128,512]{1,0:T(8,128)(2,1)}, u32[]{:S(2)}) copy-start(bf16[128,512]{1,0:T(8,128)(2,1)} %copy-done.35) | copy-start | bytes 393220
  230.3 28.7 %copy-start.19 = (f32[1,512,512]{1,2,0:T(8,128)S(1)}, f32[1,512,512]{1,2,0:T(8,128)}, u32[]{:S(2)}) copy-start(f32[1,512,512]{1,2,0:T(8,128)} %convolution_bitcast_fusion) | copy-start | bytes 3145732
  251.7 14.1 %all-to-all-start.5 = ((bf16[32,4,512]{2,1,0:T(4,128)(2,1)}), bf16[32,4,512]{2,1,0:T(4,128)(2,1)}, u32[]{:S(2)}, u32[]{:S(2)}) async-start(bf16[32,4,512]{2,1,0:T(4,128)(2,1)} %reshape.510), calls=%async_computation.5 | async-start | bytes 262144 | tf_op jit(solution)/shard_map/all_to_all | solution.py:83
  262.6 9.5 %copy-start.29 = (f32[128,512]{1,0:T(8,128)S(1)}, f32[128,512]{1,0:T(8,128)}, u32[]{:S(2)}) copy-start(f32[128,512]{1,0:T(8,128)} %copy-done.28) | copy-start | bytes 786436
  279.9 30.0 %copy-start.34 = (bf16[128,512]{1,0:T(8,128)(2,1)S(1)}, bf16[128,512]{1,0:T(8,128)(2,1)}, u32[]{:S(2)}) copy-start(bf16[128,512]{1,0:T(8,128)(2,1)} %copy-done.33) | copy-start | bytes 393220
  284.4 26.8 %copy-start.17 = (f32[1,512,512]{1,2,0:T(8,128)S(1)}, f32[1,512,512]{1,2,0:T(8,128)}, u32[]{:S(2)}) copy-start(f32[1,512,512]{1,2,0:T(8,128)} %convolution_bitcast_fusion.3) | copy-start | bytes 3145732
  305.9 12.2 %all-to-all-start.6 = ((bf16[32,4,512]{2,1,0:T(4,128)(2,1)}), bf16[32,4,512]{2,1,0:T(4,128)(2,1)}, u32[]{:S(2)}, u32[]{:S(2)}) async-start(bf16[32,4,512]{2,1,0:T(4,128)(2,1)} %reshape.511), calls=%async_computation.6 | async-start | bytes 262144 | tf_op jit(solution)/shard_map/all_to_all | solution.py:83
  311.3 9.5 %copy-start.8 = (f32[128,512]{1,0:T(8,128)S(1)}, f32[128,512]{1,0:T(8,128)}, u32[]{:S(2)}) copy-start(f32[128,512]{1,0:T(8,128)} %copy-done.7) | copy-start | bytes 786436
  311.3 9.5 %copy-start.49 = (f32[1,512]{1,0:T(1,128)S(1)}, f32[1,512]{1,0:T(1,128)}, u32[]{:S(2)}) copy-start(f32[1,512]{1,0:T(1,128)} %copy-done.48) | copy-start | bytes 6148
  311.3 9.6 %copy-start.70 = (f32[128]{0:T(128)S(1)}, f32[128]{0:T(128)}, u32[]{:S(2)}) copy-start(f32[128]{0:T(128)} %copy-done.69) | copy-start | bytes 1540
  332.0 29.8 %copy-start.38 = (bf16[128,512]{1,0:T(8,128)(2,1)S(1)}, bf16[128,512]{1,0:T(8,128)(2,1)}, u32[]{:S(2)}) copy-start(bf16[128,512]{1,0:T(8,128)(2,1)} %param.18) | copy-start | bytes 393220
  332.0 31.2 %copy-start.61 = (f32[512]{0:T(512)S(1)}, f32[512]{0:T(512)}, u32[]{:S(2)}) copy-start(f32[512]{0:T(512)} %get-tuple-element.9) | copy-start | bytes 6148
  332.0 31.1 %copy-start.62 = (f32[512]{0:T(512)S(1)}, f32[512]{0:T(512)}, u32[]{:S(2)}) copy-start(f32[512]{0:T(512)} %get-tuple-element.16) | copy-start | bytes 6148
  336.4 27.4 %copy-start.16 = (f32[1,512,512]{1,2,0:T(8,128)S(1)}, f32[1,512,512]{1,2,0:T(8,128)}, u32[]{:S(2)}) copy-start(f32[1,512,512]{1,2,0:T(8,128)} %convolution_bitcast_fusion.6) | copy-start | bytes 3145732
  336.4 27.5 %copy-start.18 = (f32[1,512,512]{1,2,0:T(8,128)S(1)}, f32[1,512,512]{1,2,0:T(8,128)}, u32[]{:S(2)}) copy-start(f32[1,512,512]{1,2,0:T(8,128)} %convolution_bitcast_fusion.7) | copy-start | bytes 3145732
  357.9 12.1 %all-to-all-start.7 = ((bf16[32,4,512]{2,1,0:T(4,128)(2,1)}), bf16[32,4,512]{2,1,0:T(4,128)(2,1)S(1)}, u32[]{:S(2)}, u32[]{:S(2)}) async-start(bf16[32,4,512]{2,1,0:T(4,128)(2,1)} %reshape.512), calls=%async_computation.7 | async-start | bytes 262144 | tf_op jit(solution)/shard_map/all_to_all | solution.py:83
  (38 other events, 170.6 us)
where the time goes:
time: 613 us; the launch traced here: 602 us
  blocking collectives  211 us (34%)
  other arithmetic  192 us (31%)
  local copies, waits for them, and re-layouts  95.8 us (16%)
  matrix products  48.4 us (8%)
  starting transfers between devices  43.1 us (7%)
  waiting for transfers between devices  8.05 us (1%)
    psum x1, blocking collectives, shards(): lax.psum((weight_stack, gain_stack), ('lat', 'lon'))  211 us
    scatter-add x4, other arithmetic, edge_forward(): jax.ops.segment_sum(hidden, receivers, num_segments=proj_recv.shape[0])  48.4 us
    all_to_all x8, starting transfers between devices, trade(): lax.all_to_all(buffer, ('lat', 'lon'), split_axis=0, concat_axis=0, tiled...  43.1 us
    scatter-add x4, other arithmetic, edge_backward(): jax.ops.segment_sum(grad_pre, senders, num_segments=slot_count)  41.9 us
    scatter-add x4, other arithmetic, edge_backward(): jax.ops.segment_sum(grad_pre, receivers, num_segments=recv_count)  41.7 us
    gather x4, local copies, waits for them, and re-layouts, edge_forward(): slot_vals[senders].astype(jnp.float32)  22 us
    gather x4, local copies, waits for them, and re-layouts, edge_forward(): proj_recv[receivers].astype(jnp.float32)  21.1 us
    unnamed x163, local copies, waits for them, and re-layouts  20.5 us
  transfers between devices with their start and end apart: 8, of which 5 were waited for; matrix products, arithmetic and copies ran while one was open for 13% of the time, Pallas kernels for 0%

commit v1 on v0

--- a/solution.py
+++ b/solution.py
@@ -215,7 +215,7 @@
     weight_parts[0], gain_parts[0] = settle(grad_weights, gain_part)
     weight_stack = jnp.stack(weight_parts)
     gain_stack = jnp.stack(gain_parts)
-    weight_stack, gain_stack = lax.psum((weight_stack, gain_stack), ("lat", "lon"))
+    weight_stack, gain_stack = lax.psum(lax.psum((weight_stack, gain_stack), "lat"), "lon")
     return (grid_out, weight_stack.astype(jnp.bfloat16), gain_stack)
 
 

time: 613 us -> 1090 us (1.78)
  waiting for transfers between devices: 8.05 us -> 420 us
  blocking collectives: 211 us -> 261 us
  between operations: 4.38 us -> 17.7 us
    psum x0 -> x1, waiting for transfers between devices: none -> 412 us  [shards(): lax.psum((weight_stack, gain_stack), 'lat')]
    psum x1 -> x2, blocking collectives: 211 us -> 261 us  [the longest x1 250 us: shards(): lax.psum(lax.psum((weight_stack, gain_stack), 'lat'), 'lon')]
  transfers between devices with their start and end apart: 8 -> 9, of which waited for: 5 -> 6; matrix products, arithmetic and copies ran while one was open for 13% -> 7% of each run, Pallas kernels for 0% -> 0%
where the time goes in v1:
time: 1090 us; the launch traced here: 1080 us
  waiting for transfers between devices  420 us (39%)
  blocking collectives  261 us (24%)
  other arithmetic  191 us (18%)
  local copies, waits for them, and re-layouts  95.7 us (9%)
  matrix products  48.4 us (4%)
  starting transfers between devices  43.1 us (4%)
  between operations  17.7 us (2%)
    psum x1, waiting for transfers between devices, shards(): lax.psum((weight_stack, gain_stack), 'lat')  412 us
    psum x1, blocking collectives, shards(): lax.psum(lax.psum((weight_stack, gain_stack), 'lat'), 'lon')  250 us
    scatter-add x4, other arithmetic, edge_forward(): jax.ops.segment_sum(hidden, receivers, num_segments=proj_recv.shape[0])  48.4 us
    all_to_all x8, starting transfers between devices, trade(): lax.all_to_all(buffer, ('lat', 'lon'), split_axis=0, concat_axis=0, tiled...  43.1 us
    scatter-add x4, other arithmetic, edge_backward(): jax.ops.segment_sum(grad_pre, senders, num_segments=slot_count)  41.9 us
    scatter-add x4, other arithmetic, edge_backward(): jax.ops.segment_sum(grad_pre, receivers, num_segments=recv_count)  41.7 us
    gather x4, local copies, waits for them, and re-layouts, edge_forward(): slot_vals[senders].astype(jnp.float32)  22 us
  transfers between devices with their start and end apart: 9, of which 6 were waited for; matrix products, arithmetic and copies ran while one was open for 7% of the time, Pallas kernels for 0%

profile of v1, /device:TPU:0, one launch (start us, length us, event | category | flops | bytes accessed | tf_op | source)
XLA Modules:
  0.0 1077.7 jit_solution(8732760198592500848)
XLA Ops:
  11.4 7.3 all-to-all-start
  25.9 4.8 gather_fusion.2
  32.3 5.4 gather_fusion.1
  37.7 11.8 %scatter_custom_fusion = f32[128,512]{1,0:T(8,128)S(1)} fusion(s32[1536]{0:T(1024)S(1)} %reduce.1, bf16[1536,512]{1,0:T(8,128)(2,1)S(1)} %gather_fusion.2, bf16[1536,512]{1,0:T(8,128)(2,1)} %gather_fusion.1, f32[1536]{0:T(1024)S(1)} %fusion.133, f32[]{:T(128)} %constant.63.clone.1, f32[]{:T(128)} %constant.59.clone.1), kind=kCustom, calls=%fused_computation.56 | custom fusion | flops 7077888 | bytes 3416072 | tf_op jit(solution)/shard_map/scatter-add | solution.py:37
  54.8 5.8 all-to-all-start.1
  62.7 5.4 gather_fusion.5
  68.9 5.4 gather_fusion.4
  74.3 11.9 %scatter_custom_fusion.1 = f32[128,512]{1,0:T(8,128)S(1)} fusion(s32[1536]{0:T(1024)S(1)} %reduce.4, bf16[1536,512]{1,0:T(8,128)(2,1)} %gather_fusion.5, bf16[1536,512]{1,0:T(8,128)(2,1)} %gather_fusion.4, f32[1536]{0:T(1024)S(1)} %fusion.134, f32[]{:T(128)} %constant.63.clone.1, f32[]{:T(128)} %constant.59.clone.1), kind=kCustom, calls=%fused_computation.51 | custom fusion | flops 7077888 | bytes 3416072 | tf_op jit(solution)/shard_map/scatter-add | solution.py:37
  91.5 5.2 all-to-all-start.2
  98.5 5.4 gather_fusion.8
  104.9 5.4 gather_fusion.7
  110.3 11.7 %scatter_custom_fusion.2 = f32[128,512]{1,0:T(8,128)S(1)} fusion(s32[1536]{0:T(1024)S(1)} %reduce.4, bf16[1536,512]{1,0:T(8,128)(2,1)} %gather_fusion.8, bf16[1536,512]{1,0:T(8,128)(2,1)} %gather_fusion.7, f32[1536]{0:T(1024)S(1)} %fusion.134, f32[]{:T(128)} %constant.63.clone.1, f32[]{:T(128)} %constant.59.clone.1), kind=kCustom, calls=%fused_computation.46 | custom fusion | flops 7077888 | bytes 3416072 | tf_op jit(solution)/shard_map/scatter-add | solution.py:37
  127.9 4.9 all-to-all-start.3
  140.7 2.1 copy.45
  142.7 5.4 gather_fusion.11
  148.8 5.7 gather_fusion.10
  154.5 13.0 %scatter_custom_fusion.3 = f32[512,512]{1,0:T(8,128)} fusion(s32[1536]{0:T(1024)} %reduce, bf16[1536,512]{1,0:T(8,128)(2,1)S(1)} %copy-done.3, bf16[1536,512]{1,0:T(8,128)(2,1)} %gather_fusion.10, f32[1536]{0:T(1024)} %fusion.135, f32[]{:T(128)} %constant.63.clone.1, f32[]{:T(128)} %constant.59.clone.1), kind=kCustom, calls=%fused_computation.41 | custom fusion | flops 7077888 | bytes 4203520 | tf_op jit(solution)/shard_map/scatter-add | solution.py:37
  173.7 4.9 gather_fusion.12
  178.7 4.9 multiply_multiply_fusion.3
  183.5 11.0 %scatter_custom_fusion.4 = f32[128,512]{1,0:T(8,128)} fusion(s32[1536]{0:T(1024)} %reduce.10, f32[1536,512]{1,0:T(8,128)} %multiply_multiply_fusion.3, f32[]{:T(128)} %constant.59.clone.1), kind=kCustom, calls=%fused_computation.206 | custom fusion | flops 786432 | bytes 262656 | tf_op jit(solution)/shard_map/scatter-add | solution.py:76
  196.1 5.8 all-to-all-start.4
  202.0 2.6 convolution_bitcast_fusion
  204.6 10.5 scatter_custom_fusion.15
  225.3 4.9 gather_fusion.13
  230.2 4.5 multiply_multiply_fusion.2
  234.8 10.4 scatter_custom_fusion.6
  245.2 10.3 scatter_custom_fusion.7
  256.2 6.0 all-to-all-start.5
  263.5 3.6 maximum_bitcast_fusion.3
  273.0 2.0 multiply_reduce_fusion.2
  279.4 4.9 gather_fusion.14
  284.3 4.5 multiply_multiply_fusion.1
  288.9 10.4 scatter_custom_fusion.9
  299.3 10.3 scatter_custom_fusion.10
  310.3 4.1 all-to-all-start.6
  315.7 3.6 maximum_bitcast_fusion.2
  331.6 4.9 gather_fusion.15
  336.5 4.4 multiply_multiply_fusion
  340.9 10.5 scatter_custom_fusion.14
  351.4 10.3 scatter_custom_fusion.12
  362.4 3.9 all-to-all-start.7
  367.7 3.4 maximum_bitcast_fusion.1
  371.1 3.4 all-to-all-done.7
  380.4 6.7 pad_maximum_fusion
  389.2 10.7 psum.30
  399.9 411.7 %all-reduce.4.cloned.1.call-done = f32[4,3,512,512]{2,3,1,0:T(8,128)} async-done(((f32[4,3,512,512]{2,3,1,0:T(8,128)}), f32[4,3,512,512]{2,3,1,0:T(8,128)}) %all-reduce.4.cloned.1.call-update) | async-done | bytes 12582928 | tf_op jit(solution)/shard_map/psum | solution.py:218
  811.6 250.3 %all-reduce.5 = (bf16[4,3,512,512]{2,3,1,0:T(8,128)(2,1)}, f32[4,512]{1,0:T(4,128)}) all-reduce(f32[4,3,512,512]{2,3,1,0:T(8,128)} %all-reduce.4.cloned.1.call-done, f32[4,512]{1,0:T(4,128)S(1)} %psum.30), channel_id=1, replica_groups=mesh['lat'=4,'lon'=8] {'lon'}, use_global_device_ids=true, to_apply=%region_33.34 | all-reduce | flops 3147776 | bytes 18890752 | tf_op jit(solution)/shard_map/psum | solution.py:218
  1061.8 8.6 copy.57
  (304 shorter events, 95.3 us)
Async XLA Ops:
  7.2 11.6 %copy-start.66 = (s32[1,32,4]{1,2,0:T(4,128)S(1)}, s32[1,32,4]{1,2,0:T(4,128)}, u32[]{:S(2)}) copy-start(s32[1,32,4]{1,2,0:T(4,128)} %param.22) | copy-start | bytes 1540
  7.2 11.7 %copy-start.67 = (s32[1,32,4]{1,2,0:T(4,128)S(1)}, s32[1,32,4]{1,2,0:T(4,128)}, u32[]{:S(2)}) copy-start(s32[1,32,4]{1,2,0:T(4,128)} %param.26) | copy-start | bytes 1540
  7.2 13.7 %copy-start.68 = (s32[1,32,4]{1,2,0:T(4,128)S(1)}, s32[1,32,4]{1,2,0:T(4,128)}, u32[]{:S(2)}) copy-start(s32[1,32,4]{1,2,0:T(4,128)} %param.30) | copy-start | bytes 1540
  7.2 14.4 %copy-start.54 = (s32[1,1536]{1,0:T(1,128)S(1)}, s32[1,1536]{1,0:T(1,128)}, u32[]{:S(2)}) copy-start(s32[1,1536]{1,0:T(1,128)} %param.24) | copy-start | bytes 18436
  7.2 14.4 %copy-start.58 = (s32[1,1536]{1,0:T(1,128)S(1)}, s32[1,1536]{1,0:T(1,128)}, u32[]{:S(2)}) copy-start(s32[1,1536]{1,0:T(1,128)} %param.23) | copy-start | bytes 18436
  7.2 14.5 %copy-start.56 = (s32[1,1536]{1,0:T(1,128)S(1)}, s32[1,1536]{1,0:T(1,128)}, u32[]{:S(2)}) copy-start(s32[1,1536]{1,0:T(1,128)} %param.27) | copy-start | bytes 18436
  7.2 14.5 %copy-start.55 = (s32[1,1536]{1,0:T(1,128)S(1)}, s32[1,1536]{1,0:T(1,128)}, u32[]{:S(2)}) copy-start(s32[1,1536]{1,0:T(1,128)} %param.28) | copy-start | bytes 18436
  7.2 14.6 %copy-start.59 = (s32[1,1536]{1,0:T(1,128)S(1)}, s32[1,1536]{1,0:T(1,128)}, u32[]{:S(2)}) copy-start(s32[1,1536]{1,0:T(1,128)} %param.31) | copy-start | bytes 18436
  7.3 14.6 %copy-start.57 = (s32[1,1536]{1,0:T(1,128)S(1)}, s32[1,1536]{1,0:T(1,128)}, u32[]{:S(2)}) copy-start(s32[1,1536]{1,0:T(1,128)} %param.32) | copy-start | bytes 18436
  7.3 15.2 %copy-start.69 = (f32[4,512]{1,0:T(4,128)S(1)}, f32[4,512]{1,0:T(4,128)}, u32[]{:S(2)}) copy-start(f32[4,512]{1,0:T(4,128)} %param.20) | copy-start | bytes 24580
  7.3 17.3 %copy-start.38 = (bf16[128,512]{1,0:T(8,128)(2,1)S(1)}, bf16[128,512]{1,0:T(8,128)(2,1)}, u32[]{:S(2)}) copy-start(bf16[128,512]{1,0:T(8,128)(2,1)} %param.18) | copy-start | bytes 393220
  11.4 20.8 %all-to-all-start = ((bf16[32,4,512]{2,1,0:T(4,128)(2,1)}), bf16[32,4,512]{2,1,0:T(4,128)(2,1)S(1)}, u32[]{:S(2)}, u32[]{:S(2)}) async-start(bf16[32,4,512]{2,1,0:T(4,128)(2,1)} %reshape.518), calls=%async_computation | async-start | bytes 262144 | tf_op jit(solution)/shard_map/all_to_all | solution.py:83
  20.9 16.7 %copy-start.42 = (f32[1536]{0:T(1024)}, f32[1536]{0:T(1024)S(1)}, u32[]{:S(2)}) copy-start(f32[1536]{0:T(1024)S(1)} %fusion.133) | copy-start | bytes 18436
  21.6 16.1 %copy-start.70 = (s32[1536]{0:T(1024)}, s32[1536]{0:T(1024)S(1)}, u32[]{:S(2)}) copy-start(s32[1536]{0:T(1024)S(1)} %reduce.1) | copy-start | bytes 18436
  23.1 28.1 %copy-start.49 = (f32[1,512]{1,0:T(1,128)}, f32[1,512]{1,0:T(1,128)S(1)}, u32[]{:S(2)}) copy-start(f32[1,512]{1,0:T(1,128)S(1)} %get-tuple-element.27) | copy-start | bytes 6148
  23.1 64.8 %copy-start.51 = (f32[1,512]{1,0:T(1,128)}, f32[1,512]{1,0:T(1,128)S(1)}, u32[]{:S(2)}) copy-start(f32[1,512]{1,0:T(1,128)S(1)} %get-tuple-element.26) | copy-start | bytes 6148
  49.5 18.7 %copy-start.26 = (f32[128,512]{1,0:T(8,128)}, f32[128,512]{1,0:T(8,128)S(1)}, u32[]{:S(2)}) copy-start(f32[128,512]{1,0:T(8,128)S(1)} %scatter_custom_fusion) | copy-start | bytes 786436
  51.9 36.0 %copy-start.34 = (bf16[128,512]{1,0:T(8,128)(2,1)}, bf16[128,512]{1,0:T(8,128)(2,1)S(1)}, u32[]{:S(2)}) copy-start(bf16[128,512]{1,0:T(8,128)(2,1)S(1)} %add_convert_fusion.3) | copy-start | bytes 393220
  54.8 14.0 %all-to-all-start.1 = ((bf16[32,4,512]{2,1,0:T(4,128)(2,1)}), bf16[32,4,512]{2,1,0:T(4,128)(2,1)S(1)}, u32[]{:S(2)}, u32[]{:S(2)}) async-start(bf16[32,4,512]{2,1,0:T(4,128)(2,1)} %reshape.542), calls=%async_computation.1 | async-start | bytes 262144 | tf_op jit(solution)/shard_map/all_to_all | solution.py:83
  61.2 49.1 %copy-start.71 = (s32[1536]{0:T(1024)}, s32[1536]{0:T(1024)S(1)}, u32[]{:S(2)}) copy-start(s32[1536]{0:T(1024)S(1)} %reduce.4) | copy-start | bytes 18436
  86.2 17.8 %copy-start.28 = (f32[128,512]{1,0:T(8,128)}, f32[128,512]{1,0:T(8,128)S(1)}, u32[]{:S(2)}) copy-start(f32[128,512]{1,0:T(8,128)S(1)} %scatter_custom_fusion.1) | copy-start | bytes 786436
  87.6 16.3 %copy-start.74 = (f32[128]{0:T(128)}, f32[128]{0:T(128)S(1)}, u32[]{:S(2)}) copy-start(f32[128]{0:T(128)S(1)} %broadcast_multiply_fusion.10) | copy-start | bytes 1540
  88.6 35.1 %copy-start.36 = (bf16[128,512]{1,0:T(8,128)(2,1)}, bf16[128,512]{1,0:T(8,128)(2,1)S(1)}, u32[]{:S(2)}) copy-start(bf16[128,512]{1,0:T(8,128)(2,1)S(1)} %add_convert_fusion.2) | copy-start | bytes 393220
  91.5 13.4 %all-to-all-start.2 = ((bf16[32,4,512]{2,1,0:T(4,128)(2,1)}), bf16[32,4,512]{2,1,0:T(4,128)(2,1)S(1)}, u32[]{:S(2)}, u32[]{:S(2)}) async-start(bf16[32,4,512]{2,1,0:T(4,128)(2,1)} %reshape.566), calls=%async_computation.2 | async-start | bytes 262144 | tf_op jit(solution)/shard_map/all_to_all | solution.py:83
  110.3 13.9 %copy-start.53 = (f32[1,512]{1,0:T(1,128)S(1)}, f32[1,512]{1,0:T(1,128)}, u32[]{:S(2)}) copy-start(f32[1,512]{1,0:T(1,128)} %get-tuple-element.28) | copy-start | bytes 6148
  122.0 20.7 %copy-start.30 = (f32[128,512]{1,0:T(8,128)}, f32[128,512]{1,0:T(8,128)S(1)}, u32[]{:S(2)}) copy-start(f32[128,512]{1,0:T(8,128)S(1)} %scatter_custom_fusion.2) | copy-start | bytes 786436
  127.9 20.8 %all-to-all-start.3 = ((bf16[32,4,512]{2,1,0:T(4,128)(2,1)}), bf16[32,4,512]{2,1,0:T(4,128)(2,1)S(1)}, u32[]{:S(2)}, u32[]{:S(2)}) async-start(bf16[32,4,512]{2,1,0:T(4,128)(2,1)} %reshape.590), calls=%async_computation.3 | async-start | bytes 262144 | tf_op jit(solution)/shard_map/all_to_all | solution.py:83
  133.6 14.6 %copy-start.47 = (s32[2048]{0:T(1024)}, s32[2048]{0:T(1024)S(1)}, u32[]{:S(2)}) copy-start(s32[2048]{0:T(1024)S(1)} %pad_clamp_fusion) | copy-start | bytes 24580
  154.5 15.2 %copy-start.60 = (f32[1,512]{1,0:T(1,128)S(1)}, f32[1,512]{1,0:T(1,128)}, u32[]{:S(2)}) copy-start(f32[1,512]{1,0:T(1,128)} %get-tuple-element.25) | copy-start | bytes 6148
  178.7 23.3 %copy-start.6 = (f32[512,512]{1,0:T(8,128)S(1)}, f32[512,512]{1,0:T(8,128)}, u32[]{:S(2)}) copy-start(f32[512,512]{1,0:T(8,128)} %scatter_custom_fusion.3) | copy-start | bytes 3145732
  183.5 31.5 %copy-start.12 = (bf16[512,512]{1,0:T(8,128)(2,1)S(1)}, bf16[512,512]{1,0:T(8,128)(2,1)}, u32[]{:S(2)}) copy-start(bf16[512,512]{1,0:T(8,128)(2,1)} %param.17) | copy-start | bytes 1572868
  196.1 20.4 %all-to-all-start.4 = ((bf16[32,4,512]{2,1,0:T(4,128)(2,1)}), bf16[32,4,512]{2,1,0:T(4,128)(2,1)S(1)}, u32[]{:S(2)}, u32[]{:S(2)}) async-start(bf16[32,4,512]{2,1,0:T(4,128)(2,1)} %reshape.509), calls=%async_computation.4 | async-start | bytes 262144 | tf_op jit(solution)/shard_map/all_to_all | solution.py:83
  230.2 31.9 %copy-start.37 = (bf16[128,512]{1,0:T(8,128)(2,1)S(1)}, bf16[128,512]{1,0:T(8,128)(2,1)}, u32[]{:S(2)}) copy-start(bf16[128,512]{1,0:T(8,128)(2,1)} %copy-done.36) | copy-start | bytes 393220
  234.8 28.8 %copy-start.19 = (f32[1,512,512]{1,2,0:T(8,128)S(1)}, f32[1,512,512]{1,2,0:T(8,128)}, u32[]{:S(2)}) copy-start(f32[1,512,512]{1,2,0:T(8,128)} %convolution_bitcast_fusion) | copy-start | bytes 3145732
  256.2 14.1 %all-to-all-start.5 = ((bf16[32,4,512]{2,1,0:T(4,128)(2,1)}), bf16[32,4,512]{2,1,0:T(4,128)(2,1)}, u32[]{:S(2)}, u32[]{:S(2)}) async-start(bf16[32,4,512]{2,1,0:T(4,128)(2,1)} %reshape.510), calls=%async_computation.5 | async-start | bytes 262144 | tf_op jit(solution)/shard_map/all_to_all | solution.py:83
  267.1 9.5 copy-start.29
  284.3 30.1 %copy-start.35 = (bf16[128,512]{1,0:T(8,128)(2,1)S(1)}, bf16[128,512]{1,0:T(8,128)(2,1)}, u32[]{:S(2)}) copy-start(bf16[128,512]{1,0:T(8,128)(2,1)} %copy-done.34) | copy-start | bytes 393220
  288.9 26.8 %copy-start.17 = (f32[1,512,512]{1,2,0:T(8,128)S(1)}, f32[1,512,512]{1,2,0:T(8,128)}, u32[]{:S(2)}) copy-start(f32[1,512,512]{1,2,0:T(8,128)} %convolution_bitcast_fusion.3) | copy-start | bytes 3145732
  310.3 12.3 %all-to-all-start.6 = ((bf16[32,4,512]{2,1,0:T(4,128)(2,1)}), bf16[32,4,512]{2,1,0:T(4,128)(2,1)}, u32[]{:S(2)}, u32[]{:S(2)}) async-start(bf16[32,4,512]{2,1,0:T(4,128)(2,1)} %reshape.511), calls=%async_computation.6 | async-start | bytes 262144 | tf_op jit(solution)/shard_map/all_to_all | solution.py:83
  315.7 9.6 copy-start.8
  315.7 9.6 copy-start.50
  315.7 9.6 copy-start.73
  319.3 9.6 copy-start.27
  336.5 29.8 %copy-start.39 = (bf16[128,512]{1,0:T(8,128)(2,1)S(1)}, bf16[128,512]{1,0:T(8,128)(2,1)}, u32[]{:S(2)}) copy-start(bf16[128,512]{1,0:T(8,128)(2,1)} %param.18) | copy-start | bytes 393220
  340.9 26.8 %copy-start.16 = (f32[1,512,512]{1,2,0:T(8,128)S(1)}, f32[1,512,512]{1,2,0:T(8,128)}, u32[]{:S(2)}) copy-start(f32[1,512,512]{1,2,0:T(8,128)} %convolution_bitcast_fusion.6) | copy-start | bytes 3145732
  340.9 26.8 %copy-start.18 = (f32[1,512,512]{1,2,0:T(8,128)S(1)}, f32[1,512,512]{1,2,0:T(8,128)}, u32[]{:S(2)}) copy-start(f32[1,512,512]{1,2,0:T(8,128)} %convolution_bitcast_fusion.7) | copy-start | bytes 3145732
  362.4 12.1 %all-to-all-start.7 = ((bf16[32,4,512]{2,1,0:T(4,128)(2,1)}), bf16[32,4,512]{2,1,0:T(4,128)(2,1)S(1)}, u32[]{:S(2)}, u32[]{:S(2)}) async-start(bf16[32,4,512]{2,1,0:T(4,128)(2,1)} %reshape.512), calls=%async_computation.7 | async-start | bytes 262144 | tf_op jit(solution)/shard_map/all_to_all | solution.py:83
  366.3 445.2 %all-reduce.4.cloned.1.call-start = ((), (), s32[]{:S(2)}) async-start(), calls=%async_computation.8 | async-start | bytes 25165824 | tf_op jit(solution)/shard_map/psum | solution.py:218
  (42 other events, 171.6 us)
Sparse Core Ops, SparseCore 0:
  387.2 424.2 all-reduce.3
